TPU v7x, 8 devices: a whole 2x2x1 slice. The times are simulated.
8 devices in a mesh: data: 8 (over z, y, x, core).
Axes of the slice: x: 2, y: 2, z: 1, core: 2. Of those that a mesh axis runs over, the one named last changes fastest.
Arguments:
- x_now: bfloat16 [128, 256, 128], P('data')
- labels_now: int32 [128], P('data')
- x_next: bfloat16 [128, 256, 128], P('data')
- up_one: float32 [2, 128, 512], replicated
- down_one: float32 [2, 512, 128], replicated
- merge_proj: float32 [512, 512], replicated
- up_two: float32 [2, 512, 2048], replicated
- down_two: float32 [2, 2048, 512], replicated
- head_proj: float32 [512, 1000], replicated
- vel_up_one: float32 [2, 128, 512], replicated
- vel_down_one: float32 [2, 512, 128], replicated
- vel_merge_proj: float32 [512, 512], replicated
- vel_up_two: float32 [2, 512, 2048], replicated
- vel_down_two: float32 [2, 2048, 512], replicated
- vel_head_proj: float32 [512, 1000], replicated
Outputs:
- output 1: float32 [128, 1000], P('data')
- output 2: float32 [2, 128, 512], replicated
- output 3: float32 [2, 512, 128], replicated
- output 4: float32 [512, 512], replicated
- output 5: float32 [2, 512, 2048], replicated
- output 6: float32 [2, 2048, 512], replicated
- output 7: float32 [512, 1000], replicated
- output 8: float32 [2, 128, 512], replicated
- output 9: float32 [2, 512, 128], replicated
- output 10: float32 [512, 512], replicated
- output 11: float32 [2, 512, 2048], replicated
- output 12: float32 [2, 2048, 512], replicated
- output 13: float32 [512, 1000], replicated
All inputs are finite; a program needn't handle non-finite values.
Results may differ from a plain program's by a relative error of at most 0.0114749.
Values are sent between devices in bfloat16 or wider.
A program may use at most 1 GiB of HBM per device.

v0:
```python
import jax
import jax.numpy as jnp
from jax import lax
from jax.experimental import pallas as pl
from jax.experimental.pallas import tpu as pltpu
from jax.sharding import PartitionSpec as P

MOMENTUM = 0.9
TRUST = 0.1
LN_EPS = 1e-6
GELU_C = 0.7978845608028654
GELU_K = 0.044715
MESH = pl.DeviceIdType.MESH
F32 = jnp.float32
BF16 = jnp.bfloat16
VMEM_LIMIT = 67043328

IMAGES = 16
TOKENS = 256
D1 = 128
H1 = 512
D2 = 512
H2 = 2048
ROWS1 = IMAGES * TOKENS
ROWS2 = ROWS1 // 4
CLASSES = 1000
CPAD = 1024
TILE = 256
NTILE = ROWS2 // TILE
WIDE = 512
CH = 7
LETTERS = 'abcdefg'
LRW = 3584
LRG = 2560
NDEV = 8
MT = 64
SUB = 8
PAIR = range(2)
QUADS = range(4)
CHUNK = 32768


def nn(a, b):
    return lax.dot_general(a, b, (((1,), (0,)), ((), ())), preferred_element_type=F32)


def nt(a, b):
    return lax.dot_general(a, b, (((1,), (1,)), ((), ())), preferred_element_type=F32)


def tn(a, b):
    return lax.dot_general(a, b, (((0,), (0,)), ((), ())), preferred_element_type=F32)


def gelu_only(x):
    inner = x * (GELU_C + (GELU_C * GELU_K) * (x * x))
    half = 0.5 + 0.5 * jnp.tanh(inner)
    return x * half


def gelu_pair(x):
    x2 = x * x
    t = jnp.tanh(x * (GELU_C + (GELU_C * GELU_K) * x2))
    half = 0.5 + 0.5 * t
    act = x * half
    slope = half + act * ((1.0 - t) * (GELU_C + (3.0 * GELU_C * GELU_K) * x2))
    return act, slope


def ln_parts(r):
    mean = jnp.mean(r, axis=-1, keepdims=True)
    cen = r - mean
    var = jnp.mean(cen * cen, axis=-1, keepdims=True)
    rstd = lax.rsqrt(var + LN_EPS)
    return cen * rstd, rstd


def ln_back(dy, xhat, rstd):
    m1 = jnp.mean(dy, axis=-1, keepdims=True)
    m2 = jnp.mean(dy * xhat, axis=-1, keepdims=True)
    return rstd * (dy - m1 - xhat * m2)


def fold_sq(v):
    rows, cols = v.shape
    s = jnp.sum((v * v).reshape(rows // SUB, SUB, cols), axis=0)
    out = s[:, 0:D1]
    for q in range(1, cols // D1):
        out = out + s[:, D1 * q:D1 * (q + 1)]
    return out


def total(acc):
    return jnp.sum(jnp.sum(acc, axis=1, keepdims=True), axis=0, keepdims=True)


def ds(start, size, mult=None):
    if isinstance(start, int):
        return pl.ds(start, size)
    return pl.ds(pl.multiple_of(start, mult or size), size)


def onehot_rows(t):
    row = lax.broadcasted_iota(jnp.int32, (IMAGES, WIDE), 0)
    col = lax.broadcasted_iota(jnp.int32, (IMAGES, WIDE), 1)
    return jnp.where(row == t * (WIDE // MT) + col // MT, 1.0, 0.0).astype(BF16)


class Ring:
    def __init__(self, num, g, r1, r2, r3, ssem, rsem, csem, pos):
        self.num = num
        self.g, self.r1, self.r2, self.r3 = (ref.at[num] for ref in (g, r1, r2, r3))
        self.ssem, self.rsem, self.csem = ssem, rsem, csem
        self.pos = pos
        self.rb = g.shape[1] // NDEV
        c, f, s = pos['c'], pos['f'], pos['s']
        self.f, self.s, self.nf, self.ns = f, s, 1 - f, 1 - s
        self.mine, self.other = 4 * c, 4 - 4 * c
        self.keep = self.mine + 2 * f
        self.give = self.mine + 2 * self.nf
        self.own_b, self.s_b = self.keep + s, self.keep + self.ns
        self.f_b, self.d_b = self.give + s, self.give + self.ns

    def blk(self, b, n=1):
        return self.g.at[ds(b * self.rb, n * self.rb, self.rb)]

    def rc(self, k, src, dst, dev):
        return pltpu.make_async_remote_copy(src_ref=src, dst_ref=dst, send_sem=self.ssem.at[self.num, k], recv_sem=self.rsem.at[self.num, k], device_id=(self.pos[dev],), device_id_type=MESH)

    def add(self, b, recv, i, n):
        rows, width = n * self.rb, self.g.shape[1]
        step = min(rows, CHUNK // width)
        b0, i0 = b * self.rb, i * self.rb

        def body(j, carry):
            dst = ds(b0 + j * step, step)
            src = ds(i0 + j * step, step)
            self.g[dst, :] = (self.g[dst, :].astype(F32) + recv[src, :].astype(F32)).astype(BF16)
            return carry

        lax.fori_loop(0, rows // step, body, 0)

    def to_core(self):
        return self.rc(0, self.blk(self.other, 4), self.r1, 'core')

    def to_f(self):
        return self.rc(1, self.blk(self.give, 2), self.r2, 'fn')

    def to_s(self):
        return self.rc(2, self.blk(self.s_b), self.r3, 'sn')

    def back(self, k, b, dev):
        return self.rc(k, self.blk(b), self.blk(b), dev)

    def own_to_s(self):
        return self.back(3, self.own_b, 'sn')

    def own_to_f(self):
        return self.back(4, self.own_b, 'fn')

    def own_to_core(self):
        return self.back(5, self.own_b, 'core')

    def s_to_f(self):
        return self.back(6, self.s_b, 'fn')

    def s_to_core(self):
        return self.back(7, self.s_b, 'core')

    def f_to_core(self):
        return self.back(8, self.f_b, 'core')

    def d_to_core(self):
        return self.back(9, self.d_b, 'core')

    def half(self):
        self.to_core().start()

    def link_f(self):
        self.to_core().wait_recv()
        self.add(self.give, self.r1, 2 * self.nf, 2)
        self.to_f().start()
        self.add(self.keep, self.r1, 2 * self.f, 2)

    def link_s(self):
        self.to_f().wait_recv()
        self.add(self.s_b, self.r2, self.ns, 1)
        self.to_s().start()
        self.add(self.own_b, self.r2, self.s, 1)
        self.to_core().wait_send()
        self.free(0, 'core')
        self.to_f().wait_send()
        self.free(1, 'fn')

    def own(self):
        self.to_s().wait_recv()
        self.to_s().wait_send()
        self.free(2, 'sn')
        self.add(self.own_b, self.r3, 0, 1)
        self.held(1)
        self.own_to_f().start()
        self.held(0)
        self.own_to_core().start()

    def own_s(self):
        self.held(2)
        self.own_to_s().start()

    def pass_s(self):
        self.own_to_s().wait_recv()
        self.s_to_f().start()
        self.s_to_core().start()

    def pass_f(self):
        self.own_to_f().wait_recv()
        self.f_to_core().start()

    def pass_d(self):
        self.s_to_f().wait_recv()
        self.d_to_core().start()

    def done(self):
        for cp in (self.own_to_core(), self.s_to_core(), self.f_to_core(), self.d_to_core()):
            cp.wait()
        for cp in (self.own_to_s(), self.own_to_f(), self.s_to_f()):
            cp.wait_send()

    def free(self, i, who):
        pl.semaphore_signal(self.csem.at[self.num, i], inc=1, device_id=(self.pos[who],), device_id_type=MESH)

    def held(self, i):
        pl.semaphore_wait(self.csem.at[self.num, i], 1)


class Share:
    def __init__(self, buf, ssem, rsem, pos):
        self.buf, self.ssem, self.rsem, self.pos = buf, ssem, rsem, pos

    def rc(self, k):
        p = self.pos
        own, fblk, sblk, dblk = p['me'], p['fn'], p['sn'], p['diag']
        b, dev = {0: (own, 'fn'), 1: (own, 'sn'), 2: (own, 'core'), 3: (fblk, 'sn'), 4: (fblk, 'core'), 5: (sblk, 'core'), 6: (dblk, 'core')}[k]
        return pltpu.make_async_remote_copy(src_ref=self.buf.at[b], dst_ref=self.buf.at[b], send_sem=self.ssem.at[k], recv_sem=self.rsem.at[k], device_id=(p[dev],), device_id_type=MESH)


    def send(self):
        for k in (0, 1, 2):
            self.rc(k).start()

    def relay(self):
        self.rc(0).wait_recv()
        self.rc(3).start()
        self.rc(4).start()
        self.rc(1).wait_recv()
        self.rc(5).start()

    def done(self):
        self.rc(3).wait_recv()
        self.rc(6).start()
        for k in (2, 4, 5, 6):
            self.rc(k).wait_recv()
        for k in range(7):
            self.rc(k).wait_send()


def position():
    me = lax.axis_index('data')
    c = lax.rem(me, 2)
    x = lax.rem(me // 2, 2)
    y = me // 4
    f = c * y + (1 - c) * x
    s = c * x + (1 - c) * y
    xn = me + 2 - 4 * x
    yn = me + 4 - SUB * y
    fn = c * yn + (1 - c) * xn
    sn = c * xn + (1 - c) * yn
    diag = xn + yn - me
    core = me + 1 - 2 * c
    return dict(me=me, c=c, f=f, s=s, fn=fn, sn=sn, diag=diag, core=core)


STEPS = ('half', 'link_f', 'link_s', 'own', 'own_s', 'pass_s', 'pass_f', 'pass_d', 'done')
SHARE_STEPS = ('send', 'relay', 'done')
PLAN = dict(
    up1=('', 'a0', '', 'b0 a1'),
    in1=('', 's1', 'b1', 'a2'),
    dn0=('', 'c0', 'b2', 'd0 a3'),
    pre0=('c1 a4', '', 'd1', 'a5 b3'),
    up0=('b4', 'e0 c2', '', 'f0 d2'),
    in0=('e1 s2', 'a6', 'f1 a7', 'c3 b5'),
    mrg=('e2 c4 d3',),
    back=('d4 f2 c5 b6', 'e3 b7 c6 a8', 'e4 f3 d5 c7', 'g0 f4 d6 b8'),
    rank=('g1 e5', 'd7', 'g2 e6 c8', 'f5 e7'),
    rankh=('g3 f6', 'g4', 'f7', 'g5'),
    tail=('d8 g6', 'e8 g7', 'f8', 'g8'),
)


def grad_kernel(x_hbm, lab, uo_hbm, do_hbm, m_hbm, ut_hbm, dt_hbm, h_hbm,
                g_out, gv1_out, gh_out, scal,
                g_all, r1_all, r2_all, r3_all, lr,
                wuo, wdo, wm, wut, wdt, wh,
                merged, n1, rst1, r2, n2, rst2, a2, sl2, pooled, asum, accv, accu, sq, gsq,
                in_sem, st_sem, out_sem, ssem, rsem, csem, lssem, lrsem):
    pos = position()
    barrier = pltpu.get_barrier_semaphore()
    for who in ('core', 'fn', 'sn'):
        pl.semaphore_signal(barrier, inc=1, device_id=(pos[who],), device_id_type=MESH)

    gv1, gh, grad = wdt.at[1], wh, r2

    share = Share(lr, lssem, lrsem, pos)
    rings = {letter: Ring(i, g_all, r1_all, r2_all, r3_all, ssem, rsem, csem, pos) for i, letter in enumerate(LETTERS)}
    outs = {letter: pltpu.make_async_copy(g_all.at[i], g_out.at[i], out_sem.at[i]) for i, letter in enumerate(LETTERS)}

    def act(word):
        letter, num = word[0], int(word[1])
        if letter == 's':
            getattr(share, SHARE_STEPS[num])()
        else:
            getattr(rings[letter], STEPS[num])()
            if STEPS[num] == 'done':
                outs[letter].start()

    def run(name, body):
        plan = PLAN[name]

        def wrapped(t, carry):
            body(t)
            for i, words in enumerate(plan):
                if words:
                    @pl.when(t == i)
                    def _():
                        for word in words.split():
                            act(word)
            return carry

        lax.fori_loop(0, len(plan), wrapped, 0)

    def forward(xb, xf, suo, sdo, sm, sut, sdt, abuf):
        loads = [pltpu.make_async_copy(src, dst, in_sem.at[i]) for i, (src, dst) in enumerate(((x_hbm, xb), (uo_hbm, suo), (do_hbm, sdo), (m_hbm, sm), (h_hbm, sdt.at[0:CLASSES])))]

        def stage_up(i):
            return pltpu.make_async_copy(ut_hbm.at[i // 2, ds((i % 2) * TILE, TILE)], sut, st_sem.at[0])

        def stage_down(i):
            return pltpu.make_async_copy(dt_hbm.at[i // 2, ds((i % 2) * ROWS2, ROWS2)], sdt, st_sem.at[1])

        for cp in loads[:3]:
            cp.start()
        stage_up(0).start()
        stage_down(0).start()
        loads[3].start()
        sq[...] = jnp.zeros_like(sq)
        for cp in loads[:3]:
            cp.wait()
        for b in PAIR:
            v = suo[b]
            sq[b] = fold_sq(v)
            wuo[b] = v.astype(BF16)
            v = sdo[b]
            sq[2 + b] = fold_sq(v)
            wdo[b] = v.astype(BF16)

        def stage_one(t, carry):
            xf[...] = xb[ds(t * ROWS2, ROWS2), :].astype(F32)
            r = jnp.concatenate([xf[pl.ds(j, TILE, stride=4), :] for j in QUADS], axis=0)
            rows = ds(t * ROWS2, ROWS2)
            for b in PAIR:
                xhat, rstd = ln_parts(r)
                n = xhat.astype(BF16)
                n1[b, rows, :] = n
                if b == 1:
                    rst1[rows, :] = rstd
                a = gelu_only(nn(n, wuo[b])).astype(BF16)
                rb = (r + nn(a, wdo[b])).astype(BF16)
                r = rb.astype(F32)
            for j in QUADS:
                merged[ds(t * TILE, TILE), D1 * j:D1 * (j + 1)] = rb[TILE * j:TILE * (j + 1), :]
            stage_up(t).wait()
            layer = t // 2

            def cast_up(i, acc):
                v = sut[ds(i * IMAGES, IMAGES), :]
                wut[layer, ds((t % 2) * TILE + i * IMAGES, IMAGES), :] = v.astype(BF16)
                return acc + fold_sq(v)

            sq[4 + layer] += lax.fori_loop(0, IMAGES, cast_up, jnp.zeros((SUB, D1), F32))
            stage_down(t).wait()

            def cast_down(i, acc):
                v = sdt[ds(i * MT, MT), :]
                wdt[layer, ds((t % 2) * ROWS2 + i * MT, MT), :] = v.astype(BF16)
                return acc + fold_sq(v)

            sq[6 + layer] += lax.fori_loop(0, IMAGES, cast_down, jnp.zeros((SUB, D1), F32))

            @pl.when(t < 3)
            def _():
                stage_up(t + 1).start()
                stage_down(t + 1).start()

            return carry

        lax.fori_loop(0, NTILE, stage_one, 0)

        loads[4].start()
        loads[3].wait()

        def cast_m(i, acc):
            v = sm[ds(i * MT, MT), :]
            wm[ds(i * MT, MT), :] = v.astype(BF16)
            return acc + fold_sq(v)

        sq[SUB] = lax.fori_loop(0, SUB, cast_m, jnp.zeros((SUB, D1), F32))

        def merge_tile(t, carry):
            rows = ds(t * WIDE, WIDE)
            r2[rows, :] = nn(merged[rows, :], wm[...]).astype(BF16)
            return carry

        lax.fori_loop(0, ROWS2 // WIDE, merge_tile, 0)
        asum[...] = jnp.zeros_like(asum)
        pooled[...] = jnp.zeros_like(pooled)

        for layer in PAIR:
            def stage_two(t, carry):
                rows = ds(t * WIDE, WIDE)
                r = r2[rows, :].astype(F32)
                xhat, rstd = ln_parts(r)
                n = xhat.astype(BF16)
                n2[layer, rows, :] = n
                rst2[layer, rows, :] = rstd
                for q in QUADS:
                    cols = slice(D2 * q, D2 * (q + 1))
                    acts, slope = gelu_pair(nn(n, wut[layer, :, cols]))
                    if layer == 0:
                        a2[rows, cols] = acts.astype(BF16)
                    else:
                        abuf[:, cols] = acts.astype(BF16)
                    sl2[layer, rows, cols] = slope.astype(BF16)
                if layer == 0:
                    r2[rows, :] = (r + nn(a2[rows, :], wdt[layer])).astype(BF16)
                else:
                    rb = (r + nn(abuf[...], wdt[layer])).astype(BF16)
                    pick = onehot_rows(t)
                    asum[...] += nn(pick, abuf[...])
                    pooled[...] += nn(pick, rb)
                return carry

            lax.fori_loop(0, ROWS2 // WIDE, stage_two, 0)
        wh[CLASSES:, :] = jnp.zeros((CPAD - CLASSES, D2), BF16)
        loads[4].wait()
        for k in QUADS:
            rows = slice(TILE * k, min(TILE * (k + 1), CLASSES))
            v = sdt[rows, :]
            wh[rows, :] = v.astype(BF16)
            sq[9] += fold_sq(v)

    pl.run_scoped(
        forward,
        pltpu.VMEM((ROWS1, D1), BF16),
        pltpu.VMEM((ROWS2, D1), F32),
        pltpu.VMEM((2, D1, H1), F32),
        pltpu.VMEM((2, H1, D1), F32),
        pltpu.VMEM((D2, D2), F32),
        pltpu.VMEM((TILE, H2), F32),
        pltpu.VMEM((ROWS2, D2), F32),
        pltpu.VMEM((WIDE, H2), BF16),
    )

    xhat, rstd = ln_parts(pooled[...] * (1.0 / MT))
    hb = xhat.astype(BF16)
    logits = nt(hb, wh[...])
    col = lax.broadcasted_iota(jnp.int32, (IMAGES, CPAD), 1)
    row = lax.broadcasted_iota(jnp.int32, (IMAGES, CPAD), 0)
    logits = jnp.where(col < CLASSES, logits, -jnp.inf)
    ex = jnp.exp(logits - jnp.max(logits, axis=-1, keepdims=True))
    prob = ex / jnp.sum(ex, axis=-1, keepdims=True)
    lab_row = jnp.zeros((IMAGES, CPAD), jnp.int32)
    for i in range(IMAGES):
        lab_row = jnp.where(row == i, lab[i], lab_row)
    gl = ((prob - jnp.where(col == lab_row, 1.0, 0.0)) * (1.0 / (IMAGES * NDEV))).astype(BF16)
    g16 = (ln_back(nn(gl, wh[...]), xhat, rstd) * (1.0 / MT)).astype(BF16)
    hi = asum[...].astype(BF16)
    lo = (asum[...] - hi.astype(F32)).astype(BF16)
    me = pos['me']
    lr[me, 0:IMAGES, 0:H2] = hi
    lr[me, IMAGES:32, 0:H2] = lo
    lr[me, 0:IMAGES, H2:LRG] = g16
    lr[me, IMAGES:32, H2:LRG] = g16
    lr[me, 0:IMAGES, LRG:LRW] = gl
    lr[me, IMAGES:32, LRG:LRG + D2] = hb
    pl.semaphore_wait(barrier, 3)
    share.send()

    asum[...] = nt(g16, wdt[1])
    pooled[...] = g16.astype(F32)

    def slope_one(i, carry):
        rows = ds(i * MT, MT)
        grad[rows, :] = jnp.broadcast_to(pooled[pl.ds(i, 1), :], (MT, D2)).astype(BF16)
        for q in QUADS:
            cols = slice(D2 * q, D2 * (q + 1))
            sl2[1, rows, cols] = (asum[pl.ds(i, 1), cols] * sl2[1, rows, cols].astype(F32)).astype(BF16)
        return carry

    lax.fori_loop(0, IMAGES, slope_one, 0)

    def up_grad(layer, first):
        def body(q):
            g_all[first + q // 2, ds((q % 2) * D2, D2), :] = tn(n2[layer], sl2[layer, :, ds(q * D2, D2)]).astype(BF16)

        return body

    def down_grad(q):
        g_all[2 + q // 2, ds((q % 2) * D2, D2), :] = tn(a2[:, ds(q * D2, D2)], grad[...]).astype(BF16)

    def input_grad(layer):
        def body(t):
            rows = ds(t * TILE, TILE)
            dy = nt(sl2[layer, rows, :], wut[layer])
            dx = ln_back(dy, n2[layer, rows, :].astype(F32), rst2[layer, rows, :])
            grad[rows, :] = (dx + grad[rows, :].astype(F32)).astype(BF16)

        return body

    def pre_grad(t):
        rows = ds(t * TILE, TILE)
        for q in QUADS:
            cols = slice(D2 * q, D2 * (q + 1))
            ga = nt(grad[rows, :], wdt[0, cols, :])
            sl2[0, rows, cols] = (ga * sl2[0, rows, cols].astype(F32)).astype(BF16)

    gsm = g_all.at[CH - 1]

    def merge_grad(t):
        gsm[D2:ROWS2, :] = tn(merged[...], grad[...]).astype(BF16)

    def stage_one_back(t):
        gm = nt(grad[ds(t * TILE, TILE), :], wm[...]).astype(BF16)
        rows = ds(t * ROWS2, ROWS2)
        g = jnp.concatenate([gm[:, D1 * j:D1 * (j + 1)] for j in QUADS], axis=0)
        for b in (1, 0):
            n = n1[b, rows, :]
            acts, slope = gelu_pair(nn(n, wuo[b]))
            accv[b] += tn(acts.astype(BF16), g)
            gp = (nt(g, wdo[b]) * slope).astype(BF16)
            accu[b] += tn(n, gp)
            if b == 1:
                dx = ln_back(nt(gp, wuo[b]), n.astype(F32), rst1[rows, :])
                g = (dx + g.astype(F32)).astype(BF16)

        @pl.when(t == 3)
        def _():
            for b in PAIR:
                gsm[D1 * b:D1 * (b + 1), :] = accu[b].astype(BF16)
                for q in PAIR:
                    gsm[TILE:D2, TILE * b + D1 * q:TILE * b + D1 * (q + 1)] = accv[b, TILE * q:TILE * (q + 1), :].astype(BF16)

    run('up1', up_grad(1, 0))
    run('in1', input_grad(1))
    run('dn0', down_grad)
    run('pre0', pre_grad)
    run('up0', up_grad(0, 4))
    run('in0', input_grad(0))
    accv[...] = jnp.zeros_like(accv)
    accu[...] = jnp.zeros_like(accu)
    gsq[...] = jnp.zeros_like(gsq)
    run('mrg', merge_grad)
    run('back', stage_one_back)

    def v1_rows(i):
        cols = ds(i * D2, D2)
        out = jnp.zeros((D2, D2), F32)
        for d in range(NDEV):
            out = out + tn(lr[d, :, cols], lr[d, :, H2:LRG]).astype(BF16).astype(F32)
        ob = out.astype(BF16)
        gv1[cols, :] = ob
        gsq[7] += fold_sq(ob.astype(F32))

    def head_rows(i):
        rows = ds(i * TILE, TILE)
        out = jnp.zeros((TILE, D2), F32)
        for d in range(NDEV):
            out = out + tn(lr[d, 0:IMAGES, ds(LRG + i * TILE, TILE, TILE)], lr[d, IMAGES:32, LRG:LRG + D2]).astype(BF16).astype(F32)
        ob = out.astype(BF16)
        gh[rows, :] = ob
        gsq[9] += fold_sq(ob.astype(F32))

    def norm_of(letter, row):
        ref = g_all.at[LETTERS.index(letter)]

        def body(i, acc):
            return acc + fold_sq(ref[ds(i * MT, MT), :].astype(F32))

        gsq[row] += lax.fori_loop(0, ROWS2 // MT, body, jnp.zeros((SUB, D1), F32))

    gv1_cp = pltpu.make_async_copy(gv1, gv1_out, out_sem.at[CH])
    gh_cp = pltpu.make_async_copy(gh, gh_out, out_sem.at[CH + 1])
    run('rank', v1_rows)
    gv1_cp.start()
    run('rankh', head_rows)
    gh_cp.start()
    norm_of('a', 5)
    norm_of('b', 5)
    norm_of('c', 6)
    for i, words in enumerate(PLAN['tail']):
        for word in words.split():
            act(word)
        if i == 0:
            norm_of('d', 6)
        if i == 1:
            norm_of('e', 4)
        if i == 2:
            norm_of('f', 4)
    for b in PAIR:
        gsq[b] = fold_sq(gsm[D1 * b:D1 * (b + 1), :].astype(F32))
        gsq[2 + b] = fold_sq(gsm[TILE:D2, TILE * b:TILE * (b + 1)].astype(F32))
    gsq[SUB] = fold_sq(gsm[D2:ROWS2, :].astype(F32))
    for i in range(10):
        ratio = jnp.sqrt(total(sq[i])) / jnp.sqrt(total(gsq[i]))
        scal[i:i + 1, :] = jnp.broadcast_to(TRUST * ratio, (1, D1))
    scal[10:IMAGES, :] = jnp.zeros((6, D1), F32)
    for letter in LETTERS:
        outs[letter].wait()
    gv1_cp.wait()
    gh_cp.wait()


def step_kernel(x_hbm, uo_hbm, do_hbm, m_hbm, ut_hbm, dt_hbm, h_hbm, vuo_hbm, vdo_hbm, vm_hbm, vut_hbm, vdt_hbm, vh_hbm,
                g_hbm, gv1_hbm, gh_hbm, scal,
                logits_out, uo_out, do_out, m_out, ut_out, dt_out, h_out, vuo_out, vdo_out, vm_out, vut_out, vdt_out, vh_out,
                xb, xf, g_all, gv1, gh, suo, sdo, sm, sh, sut, sdt, tuo, tdo, tm, th, tut, tdt,
                wuo, wdo, wm, wut, wdt, wh, r2, pooled,
                s_in, s_out, q_in, q_out, g_sem):
    small = [(uo_hbm, suo, uo_out), (vuo_hbm, tuo, vuo_out), (do_hbm, sdo, do_out), (vdo_hbm, tdo, vdo_out), (m_hbm, sm, m_out), (vm_hbm, tm, vm_out), (h_hbm, sh, h_out), (vh_hbm, th, vh_out)]
    ins = [pltpu.make_async_copy(src, buf, s_in.at[i]) for i, (src, buf, _) in enumerate(small)]
    louts = [pltpu.make_async_copy(buf, dst, s_out.at[i]) for i, (_, buf, dst) in enumerate(small)]
    big = [(ut_hbm, sut, ut_out, D1), (vut_hbm, tut, vut_out, D1), (dt_hbm, sdt, dt_out, D2), (vdt_hbm, tdt, vdt_out, D2)]
    gsm = g_all.at[CH - 1]

    def qin(layer, t, k):
        src, buf, _, n = big[k]
        return pltpu.make_async_copy(src.at[layer, ds(t * n, n)], buf.at[ds(t * n, n)], q_in.at[k, t])

    def qout(layer, t, k):
        _, buf, dst, n = big[k]
        return pltpu.make_async_copy(buf.at[ds(t * n, n)], dst.at[layer, ds(t * n, n)], q_out.at[k, t])

    x_cp = pltpu.make_async_copy(x_hbm, xb, g_sem.at[CH])
    g_cps = [pltpu.make_async_copy(g_hbm.at[i], g_all.at[i], g_sem.at[i]) for i in range(CH)]
    gv1_cp = pltpu.make_async_copy(gv1_hbm, gv1, g_sem.at[CH + 1])
    gh_cp = pltpu.make_async_copy(gh_hbm, gh, g_sem.at[CH + 2])
    x_cp.start()
    g_cps[CH - 1].start()
    for cp in ins[:4]:
        cp.start()

    def update(w, v, g, scale):
        nv = MOMENTUM * v + scale * g.astype(F32)
        nw = w - nv
        return nw, nv

    x_cp.wait()
    g_cps[CH - 1].wait()
    for cp in ins[:4]:
        cp.wait()
    for i in (4, 5, 2, 3):
        g_cps[i].start()
    for t in QUADS:
        for k in QUADS:
            qin(0, t, k).start()
    ins[4].start()
    ins[5].start()
    g_cps[0].start()
    g_cps[1].start()
    gv1_cp.start()
    gh_cp.start()
    ins[6].start()
    ins[7].start()
    for b in PAIR:
        nw, nv = update(suo[b], tuo[b], gsm[D1 * b:D1 * (b + 1), :], scal[b:b + 1, 0:1])
        suo[b] = nw
        tuo[b] = nv
        wuo[b] = nw.astype(BF16)
        for q in PAIR:
            rows = slice(TILE * q, TILE * (q + 1))
            nw, nv = update(sdo[b, rows, :], tdo[b, rows, :], gsm[TILE:D2, TILE * b + D1 * q:TILE * b + D1 * (q + 1)], scal[2 + b:3 + b, 0:1])
            sdo[b, rows, :] = nw
            tdo[b, rows, :] = nv
            wdo[b, rows, :] = nw.astype(BF16)
    for cp in louts[:4]:
        cp.start()

    def loop_update(wbuf, vbuf, gref, wdst, base, count, scale, gbase):
        def body(i, carry):
            rows = ds(base + i * MT, MT)
            nw, nv = update(wbuf[rows, :], vbuf[rows, :], gref[ds(gbase + i * MT, MT), :], scale)
            wbuf[rows, :] = nw
            vbuf[rows, :] = nv
            wdst[rows, :] = nw.astype(BF16)
            return carry

        lax.fori_loop(0, count // MT, body, 0)

    def big_update(layer, t):
        for k in QUADS:
            qin(layer, t, k).wait()
        up_scale, down_scale = scal[4 + layer:5 + layer, 0:1], scal[6 + layer:7 + layer, 0:1]

        def up_body(i, carry):
            rows = ds(t * D1 + i * IMAGES, IMAGES)
            for q in QUADS:
                cols = slice(D2 * q, D2 * (q + 1))
                g = g_all[4 - 4 * layer + q // 2, ds((q % 2) * D2 + t * D1 + i * IMAGES, IMAGES), :]
                nw, nv = update(sut[rows, cols], tut[rows, cols], g, up_scale)
                sut[rows, cols] = nw
                tut[rows, cols] = nv
                wut[layer, rows, cols] = nw.astype(BF16)
            return carry

        lax.fori_loop(0, D1 // IMAGES, up_body, 0)
        if layer == 0:
            loop_update(sdt, tdt, g_all.at[2 + t // 2], wdt.at[0], t * D2, D2, down_scale, (t % 2) * D2)
        else:
            loop_update(sdt, tdt, gv1, wdt.at[1], t * D2, D2, down_scale, t * D2)
        for k in QUADS:
            qout(layer, t, k).start()

    def refill(t):
        for k in QUADS:
            qout(0, t, k).wait()
        for k in QUADS:
            qin(1, t, k).start()

    def stage_one(t, carry):
        xf[...] = xb[ds(t * ROWS2, ROWS2), :].astype(F32)
        r = jnp.concatenate([xf[pl.ds(j, TILE, stride=4), :] for j in QUADS], axis=0)
        for b in PAIR:
            xhat, _ = ln_parts(r)
            a = gelu_only(nn(xhat.astype(BF16), wuo[b])).astype(BF16)
            rb = (r + nn(a, wdo[b])).astype(BF16)
            r = rb.astype(F32)
        for j in QUADS:
            r2[ds(t * TILE, TILE), D1 * j:D1 * (j + 1)] = rb[TILE * j:TILE * (j + 1), :]

        @pl.when(t == 0)
        def _():
            for i in (4, 5, 2, 3):
                g_cps[i].wait()

        big_update(0, t)

        @pl.when(t > 0)
        def _():
            refill(t - 1)

        return carry

    lax.fori_loop(0, NTILE, stage_one, 0)
    for cp in ins[4:6]:
        cp.wait()
    loop_update(sm, tm, gsm.at[D2:ROWS2], wm, 0, D2, scal[SUB:9, 0:1], 0)
    for cp in louts[4:6]:
        cp.start()
    refill(3)
    g_cps[0].wait()
    g_cps[1].wait()
    gv1_cp.wait()
    pooled[...] = jnp.zeros_like(pooled)

    def stage_two(layer, r):
        xhat, _ = ln_parts(r)
        n = xhat.astype(BF16)
        acc = r
        for q in QUADS:
            cols = slice(D2 * q, D2 * (q + 1))
            a = gelu_only(nn(n, wut[layer, :, cols])).astype(BF16)
            acc = acc + nn(a, wdt[layer, cols, :])
        return acc.astype(BF16)

    def first(t, carry):
        rows = ds(t * WIDE, WIDE)
        r = nn(r2[rows, :], wm[...]).astype(BF16).astype(F32)
        r2[rows, :] = stage_two(0, r)

        def both(i, inner):
            big_update(1, 2 * t + i)
            return inner

        lax.fori_loop(0, 2, both, 0)
        return carry

    lax.fori_loop(0, ROWS2 // WIDE, first, 0)

    wh[CLASSES:, :] = jnp.zeros((CPAD - CLASSES, D2), BF16)
    ins[6].wait()
    ins[7].wait()
    gh_cp.wait()
    for k in QUADS:
        rows = slice(TILE * k, min(TILE * (k + 1), CLASSES))
        nw, nv = update(sh[rows, :], th[rows, :], gh[rows, :], scal[9:10, 0:1])
        sh[rows, :] = nw
        th[rows, :] = nv
        wh[rows, :] = nw.astype(BF16)
    for cp in louts[6:]:
        cp.start()

    def second(t, carry):
        rows = ds(t * WIDE, WIDE)
        rb = stage_two(1, r2[rows, :].astype(F32))
        pooled[...] += nn(onehot_rows(t), rb)
        return carry

    lax.fori_loop(0, ROWS2 // WIDE, second, 0)
    xhat, _ = ln_parts(pooled[...] * (1.0 / MT))
    logits = nt(xhat.astype(BF16), wh[...])
    logits_out[...] = logits[:, 0:CLASSES]
    for cp in louts:
        cp.wait()
    for t in QUADS:
        for k in QUADS:
            qout(1, t, k).wait()


def weight_scratch():
    return [pltpu.VMEM((2, D1, H1), BF16), pltpu.VMEM((2, H1, D1), BF16), pltpu.VMEM((D2, D2), BF16), pltpu.VMEM((2, D2, H2), BF16), pltpu.VMEM((2, H2, D2), BF16), pltpu.VMEM((CPAD, D2), BF16)]


def master_scratch():
    return [pltpu.VMEM((2, D1, H1), F32), pltpu.VMEM((2, H1, D1), F32), pltpu.VMEM((D2, D2), F32), pltpu.VMEM((CLASSES, D2), F32), pltpu.VMEM((D2, H2), F32), pltpu.VMEM((H2, D2), F32)]


def solution(mesh):
    hbm = pl.BlockSpec(memory_space=pl.ANY)
    vmem = pl.BlockSpec(memory_space=pltpu.VMEM)
    smem = pl.BlockSpec(memory_space=pltpu.SMEM)
    shape = jax.ShapeDtypeStruct
    dma = pltpu.SemaphoreType.DMA
    wide_g = [shape((CH, ROWS2, D2), BF16), shape((H2, D2), BF16), shape((CPAD, D2), BF16)]
    masters = [shape((2, D1, H1), F32), shape((2, H1, D1), F32), shape((D2, D2), F32), shape((2, D2, H2), F32), shape((2, H2, D2), F32), shape((CLASSES, D2), F32)]

    grads_call = pl.pallas_call(
        grad_kernel,
        out_shape=wide_g + [shape((IMAGES, D1), F32)],
        in_specs=[hbm, smem] + [hbm] * 6,
        out_specs=[hbm] * 3 + [vmem],
        scratch_shapes=[pltpu.VMEM((CH, ROWS2 // k, D2), BF16) for k in (1, 2, 4, NDEV)]
        + [pltpu.VMEM((NDEV, 32, LRW), BF16)]
        + weight_scratch()
        + [pltpu.VMEM((ROWS2, D2), BF16), pltpu.VMEM((2, ROWS1, D1), BF16), pltpu.VMEM((ROWS1, 1), F32), pltpu.VMEM((ROWS2, D2), BF16), pltpu.VMEM((2, ROWS2, D2), BF16), pltpu.VMEM((2, ROWS2, 1), F32), pltpu.VMEM((ROWS2, H2), BF16), pltpu.VMEM((2, ROWS2, H2), BF16), pltpu.VMEM((IMAGES, D2), F32), pltpu.VMEM((IMAGES, H2), F32), pltpu.VMEM((2, H1, D1), F32), pltpu.VMEM((2, D1, H1), F32), pltpu.VMEM((10, SUB, D1), F32), pltpu.VMEM((10, SUB, D1), F32)]
        + [dma((5,)), dma((2,)), dma((CH + 2,)), dma((CH, 10)), dma((CH, 10)), pltpu.SemaphoreType.REGULAR((CH, 3)), dma((CH,)), dma((CH,))],
        compiler_params=pltpu.CompilerParams(collective_id=0, has_side_effects=True, vmem_limit_bytes=VMEM_LIMIT),
        name="grads",
    )

    step_call = pl.pallas_call(
        step_kernel,
        out_shape=[shape((IMAGES, CLASSES), F32)] + masters * 2,
        in_specs=[hbm] * 16 + [vmem],
        out_specs=[vmem] + [hbm] * 12,
        scratch_shapes=[pltpu.VMEM((ROWS1, D1), BF16), pltpu.VMEM((ROWS2, D1), F32)]
        + [pltpu.VMEM(g.shape, BF16) for g in wide_g]
        + master_scratch() * 2
        + weight_scratch()
        + [pltpu.VMEM((ROWS2, D2), BF16), pltpu.VMEM((IMAGES, D2), F32)]
        + [dma((SUB,)), dma((SUB,)), dma((4, 4)), dma((4, 4)), dma((CH + 3,))],
        compiler_params=pltpu.CompilerParams(vmem_limit_bytes=VMEM_LIMIT),
        name="step",
    )

    def local_step(x_now, labels_now, x_next, up_one, down_one, merge_proj, up_two, down_two, head_proj, vel_up_one, vel_down_one, vel_merge_proj, vel_up_two, vel_down_two, vel_head_proj):
        params = (up_one, down_one, merge_proj, up_two, down_two, head_proj.T)
        vels = (vel_up_one, vel_down_one, vel_merge_proj, vel_up_two, vel_down_two, vel_head_proj.T)
        got = grads_call(x_now.reshape(ROWS1, D1), labels_now, *params)
        outs = list(step_call(x_next.reshape(ROWS1, D1), *params, *vels, *got))
        outs[6], outs[12] = outs[6].T, outs[12].T
        return tuple(outs)

    replicated = P()
    batch_split = P('data')
    in_specs = (batch_split, batch_split, batch_split) + (replicated,) * 12
    out_specs = (batch_split,) + (replicated,) * 12
    return jax.shard_map(local_step, mesh=mesh, in_specs=in_specs, out_specs=out_specs, check_vma=False)
```

profile of v0, /device:TPU:0, one launch (start us, length us, event | category | flops | bytes accessed | tf_op | source)
XLA Modules:
  0.0 158.1 jit_solution(5164072070128986655)
XLA Ops:
  0.6 116.7 %grads.1 = (bf16[7,1024,512]{2,1,0:T(8,128)(2,1)}, bf16[2048,512]{1,0:T(8,128)(2,1)}, bf16[1024,512]{1,0:T(8,128)(2,1)}, f32[16,128]{1,0:T(8,128)}) custom-call(bf16[4096,128]{1,0:T(8,128)(2,1)} %bitcast.9, s32[16]{0:T(128)} %lab.1, f32[2,128,512]{2,1,0:T(8,128)} %uo_hbm.3, f32[2,512,128]{2,1,0:T(8,128)} %do_hbm.3, f32[512,512]{1,0:T(8,128)} %m_hbm.3, ...), custom_call_target="tpu_custom_call" | custom-call | tf_op jit(solution)/shard_map/grads/pallas_call | solution.py:876
  117.3 40.6 %step.1 = (f32[16,1000]{1,0:T(8,128)}, f32[2,128,512]{2,1,0:T(8,128)}, f32[2,512,128]{2,1,0:T(8,128)}, f32[512,512]{1,0:T(8,128)}, f32[2,512,2048]{2,1,0:T(8,128...) custom-call(bf16[4096,128]{1,0:T(8,128)(2,1)} %bitcast.10, ...), custom_call_target="tpu_custom_call" | custom-call | tf_op jit(solution)/shard_map/step/pallas_call | solution.py:877
where the time goes:
time: 158 us
  Pallas kernels  157 us (99%)
    pallas_call x1, Pallas kernels, local_step(): got = grads_call(x_now.reshape(ROWS1, D1), labels_now, *params)  117 us
    pallas_call x1, Pallas kernels, local_step(): outs = list(step_call(x_next.reshape(ROWS1, D1), *params, *vels, *got))  40.6 us

commit v1 on v0

--- a/solution.py
+++ b/solution.py
@@ -28,15 +28,18 @@
 TILE = 256
 NTILE = ROWS2 // TILE
 WIDE = 512
+HEAD_STEP = 192
 CH = 7
 LETTERS = 'abcdefg'
-LRW = 3584
+NORM_ROW = dict(a=5, b=5, c=6, d=6, e=4, f=4)
+LRW = 3072
 LRG = 2560
 NDEV = 8
 MT = 64
 SUB = 8
 PAIR = range(2)
 QUADS = range(4)
+DOWNS = (2, 3)
 CHUNK = 32768
 
 
@@ -104,6 +107,24 @@
     row = lax.broadcasted_iota(jnp.int32, (IMAGES, WIDE), 0)
     col = lax.broadcasted_iota(jnp.int32, (IMAGES, WIDE), 1)
     return jnp.where(row == t * (WIDE // MT) + col // MT, 1.0, 0.0).astype(BF16)
+
+
+def stage_one_tile(t, xb, xf, wuo, wdo, dst):
+    xf[...] = xb[ds(t * ROWS2, ROWS2), :].astype(F32)
+    r = jnp.concatenate([xf[pl.ds(j, TILE, stride=4), :] for j in QUADS], axis=0)
+    for b in PAIR:
+        xhat, _ = ln_parts(r)
+        a = gelu_only(nn(xhat.astype(BF16), wuo[b])).astype(BF16)
+        rb = (r + nn(a, wdo[b])).astype(BF16)
+        r = rb.astype(F32)
+    for j in QUADS:
+        dst[ds(t * TILE, TILE), D1 * j:D1 * (j + 1)] = rb[TILE * j:TILE * (j + 1), :]
+
+
+def update(w, v, g, scale):
+    nv = MOMENTUM * v + scale * g.astype(F32)
+    nw = w - nv
+    return nw, nv
 
 
 class Ring:
@@ -282,23 +303,23 @@
 STEPS = ('half', 'link_f', 'link_s', 'own', 'own_s', 'pass_s', 'pass_f', 'pass_d', 'done')
 SHARE_STEPS = ('send', 'relay', 'done')
 PLAN = dict(
-    up1=('', 'a0', '', 'b0 a1'),
-    in1=('', 's1', 'b1', 'a2'),
-    dn0=('', 'c0', 'b2', 'd0 a3'),
-    pre0=('c1 a4', '', 'd1', 'a5 b3'),
-    up0=('b4', 'e0 c2', '', 'f0 d2'),
-    in0=('e1 s2', 'a6', 'f1 a7', 'c3 b5'),
-    mrg=('e2 c4 d3',),
-    back=('d4 f2 c5 b6', 'e3 b7 c6 a8', 'e4 f3 d5 c7', 'g0 f4 d6 b8'),
-    rank=('g1 e5', 'd7', 'g2 e6 c8', 'f5 e7'),
-    rankh=('g3 f6', 'g4', 'f7', 'g5'),
-    tail=('d8 g6', 'e8 g7', 'f8', 'g8'),
+    up1=((), ('a0',), (), ('b0',),),
+    in1=(('a1',), ('s1',), ('b1',), (),),
+    dn0=((), ('c0',), (), ('d0',),),
+    pre0=(('a2', 'c1', 's2',), ('d1',), (), ('b2',),),
+    up0=((), ('a3', 'e0',), (), ('a4', 'f0',),),
+    in0=(('e1', 'c2', 'b3',), ('f1', 'b4',), (), ('a5',),),
+    mrg=((),),
+    back=(('a6', 'c3', 'd2',), ('b5', 'c4', 'e2',), ('b6', 'd3',), ('c5', 'd4', 'e3', 'a7', 'f2', 'g0',),),
+    rank=(('c6', 'a8', 'e4',), ('g1', 'b7',), ('d5',), ('b8', 'd6',),),
+    rankh=((), ('f3',), (), ('c7', 'f4',),),
+    tail=('e5', 'e6', 'c8', 'f5', 'g2', 'd7', 'd8', 'f6', 'g3', 'e7', 'g4', 'f7', 'e8', 'f8', 'g5', 'g6', 'g7', 'g8', ),
 )
 
 
 def grad_kernel(x_hbm, lab, uo_hbm, do_hbm, m_hbm, ut_hbm, dt_hbm, h_hbm,
                 g_out, gv1_out, gh_out, scal,
-                g_all, r1_all, r2_all, r3_all, lr,
+                g_all, r1_all, r2_all, r3_all, lr, gdup,
                 wuo, wdo, wm, wut, wdt, wh,
                 merged, n1, rst1, r2, n2, rst2, a2, sl2, pooled, asum, accv, accu, sq, gsq,
                 in_sem, st_sem, out_sem, ssem, rsem, csem, lssem, lrsem):
@@ -312,6 +333,14 @@
     share = Share(lr, lssem, lrsem, pos)
     rings = {letter: Ring(i, g_all, r1_all, r2_all, r3_all, ssem, rsem, csem, pos) for i, letter in enumerate(LETTERS)}
     outs = {letter: pltpu.make_async_copy(g_all.at[i], g_out.at[i], out_sem.at[i]) for i, letter in enumerate(LETTERS)}
+
+    def norm_of(letter):
+        ref = g_all.at[LETTERS.index(letter)]
+
+        def body(i, acc):
+            return acc + fold_sq(ref[ds(i * MT, MT), :].astype(F32))
+
+        gsq[NORM_ROW[letter]] += lax.fori_loop(0, ROWS2 // MT, body, jnp.zeros((SUB, D1), F32))
 
     def act(word):
         letter, num = word[0], int(word[1])
@@ -321,6 +350,8 @@
             getattr(rings[letter], STEPS[num])()
             if STEPS[num] == 'done':
                 outs[letter].start()
+                if letter in NORM_ROW:
+                    norm_of(letter)
 
     def run(name, body):
         plan = PLAN[name]
@@ -331,7 +362,7 @@
                 if words:
                     @pl.when(t == i)
                     def _():
-                        for word in words.split():
+                        for word in words:
                             act(word)
             return carry
 
@@ -377,23 +408,23 @@
                 r = rb.astype(F32)
             for j in QUADS:
                 merged[ds(t * TILE, TILE), D1 * j:D1 * (j + 1)] = rb[TILE * j:TILE * (j + 1), :]
+            layer = t // 2
             stage_up(t).wait()
-            layer = t // 2
 
             def cast_up(i, acc):
-                v = sut[ds(i * IMAGES, IMAGES), :]
-                wut[layer, ds((t % 2) * TILE + i * IMAGES, IMAGES), :] = v.astype(BF16)
+                v = sut[ds(i * 32, 32), :]
+                wut[layer, ds((t % 2) * TILE + i * 32, 32), :] = v.astype(BF16)
                 return acc + fold_sq(v)
 
-            sq[4 + layer] += lax.fori_loop(0, IMAGES, cast_up, jnp.zeros((SUB, D1), F32))
+            sq[4 + layer] += lax.fori_loop(0, SUB, cast_up, jnp.zeros((SUB, D1), F32))
             stage_down(t).wait()
 
             def cast_down(i, acc):
-                v = sdt[ds(i * MT, MT), :]
-                wdt[layer, ds((t % 2) * ROWS2 + i * MT, MT), :] = v.astype(BF16)
+                v = sdt[ds(i * D1, D1), :]
+                wdt[layer, ds((t % 2) * ROWS2 + i * D1, D1), :] = v.astype(BF16)
                 return acc + fold_sq(v)
 
-            sq[6 + layer] += lax.fori_loop(0, IMAGES, cast_down, jnp.zeros((SUB, D1), F32))
+            sq[6 + layer] += lax.fori_loop(0, SUB, cast_down, jnp.zeros((SUB, D1), F32))
 
             @pl.when(t < 3)
             def _():
@@ -488,9 +519,9 @@
     lr[me, 0:IMAGES, 0:H2] = hi
     lr[me, IMAGES:32, 0:H2] = lo
     lr[me, 0:IMAGES, H2:LRG] = g16
-    lr[me, IMAGES:32, H2:LRG] = g16
-    lr[me, 0:IMAGES, LRG:LRW] = gl
-    lr[me, IMAGES:32, LRG:LRG + D2] = hb
+    lr[me, IMAGES:32, H2:LRG] = hb
+    lr[me, 0:IMAGES, LRG:LRW] = gl[:, 0:D2]
+    lr[me, IMAGES:32, LRG:LRW] = gl[:, D2:CPAD]
     pl.semaphore_wait(barrier, 3)
     share.send()
 
@@ -574,7 +605,7 @@
         cols = ds(i * D2, D2)
         out = jnp.zeros((D2, D2), F32)
         for d in range(NDEV):
-            out = out + tn(lr[d, :, cols], lr[d, :, H2:LRG]).astype(BF16).astype(F32)
+            out = out + tn(lr[d, :, cols], gdup[d]).astype(BF16).astype(F32)
         ob = out.astype(BF16)
         gv1[cols, :] = ob
         gsq[7] += fold_sq(ob.astype(F32))
@@ -583,37 +614,23 @@
         rows = ds(i * TILE, TILE)
         out = jnp.zeros((TILE, D2), F32)
         for d in range(NDEV):
-            out = out + tn(lr[d, 0:IMAGES, ds(LRG + i * TILE, TILE, TILE)], lr[d, IMAGES:32, LRG:LRG + D2]).astype(BF16).astype(F32)
+            gl_d = lr[d, ds((i // 2) * IMAGES, IMAGES), ds(LRG + (i % 2) * TILE, TILE)]
+            out = out + tn(gl_d, lr[d, IMAGES:32, H2:LRG]).astype(BF16).astype(F32)
         ob = out.astype(BF16)
         gh[rows, :] = ob
         gsq[9] += fold_sq(ob.astype(F32))
 
-    def norm_of(letter, row):
-        ref = g_all.at[LETTERS.index(letter)]
-
-        def body(i, acc):
-            return acc + fold_sq(ref[ds(i * MT, MT), :].astype(F32))
-
-        gsq[row] += lax.fori_loop(0, ROWS2 // MT, body, jnp.zeros((SUB, D1), F32))
-
     gv1_cp = pltpu.make_async_copy(gv1, gv1_out, out_sem.at[CH])
     gh_cp = pltpu.make_async_copy(gh, gh_out, out_sem.at[CH + 1])
+    for d in range(NDEV):
+        gdup[d, 0:IMAGES, :] = lr[d, 0:IMAGES, H2:LRG]
+        gdup[d, IMAGES:32, :] = lr[d, 0:IMAGES, H2:LRG]
     run('rank', v1_rows)
     gv1_cp.start()
     run('rankh', head_rows)
     gh_cp.start()
-    norm_of('a', 5)
-    norm_of('b', 5)
-    norm_of('c', 6)
-    for i, words in enumerate(PLAN['tail']):
-        for word in words.split():
-            act(word)
-        if i == 0:
-            norm_of('d', 6)
-        if i == 1:
-            norm_of('e', 4)
-        if i == 2:
-            norm_of('f', 4)
+    for word in PLAN['tail']:
+        act(word)
     for b in PAIR:
         gsq[b] = fold_sq(gsm[D1 * b:D1 * (b + 1), :].astype(F32))
         gsq[2 + b] = fold_sq(gsm[TILE:D2, TILE * b:TILE * (b + 1)].astype(F32))
@@ -637,138 +654,54 @@
     small = [(uo_hbm, suo, uo_out), (vuo_hbm, tuo, vuo_out), (do_hbm, sdo, do_out), (vdo_hbm, tdo, vdo_out), (m_hbm, sm, m_out), (vm_hbm, tm, vm_out), (h_hbm, sh, h_out), (vh_hbm, th, vh_out)]
     ins = [pltpu.make_async_copy(src, buf, s_in.at[i]) for i, (src, buf, _) in enumerate(small)]
     louts = [pltpu.make_async_copy(buf, dst, s_out.at[i]) for i, (_, buf, dst) in enumerate(small)]
-    big = [(ut_hbm, sut, ut_out, D1), (vut_hbm, tut, vut_out, D1), (dt_hbm, sdt, dt_out, D2), (vdt_hbm, tdt, vdt_out, D2)]
+    up_big = [(ut_hbm, sut, ut_out), (vut_hbm, tut, vut_out)]
+    down_big = [(dt_hbm, sdt, dt_out), (vdt_hbm, tdt, vdt_out)]
     gsm = g_all.at[CH - 1]
 
-    def qin(layer, t, k):
-        src, buf, _, n = big[k]
-        return pltpu.make_async_copy(src.at[layer, ds(t * n, n)], buf.at[ds(t * n, n)], q_in.at[k, t])
-
-    def qout(layer, t, k):
-        _, buf, dst, n = big[k]
-        return pltpu.make_async_copy(buf.at[ds(t * n, n)], dst.at[layer, ds(t * n, n)], q_out.at[k, t])
+    def copies(layer, t, into, which=QUADS):
+        out = []
+        for k in which:
+            src, buf, dst = (up_big + down_big)[k]
+            n = D1 if k in PAIR else D2
+            rows = ds(t * n, n)
+            here = buf.at[rows] if k in PAIR else buf.at[layer, rows]
+            if into:
+                out.append(pltpu.make_async_copy(src.at[layer, rows], here, q_in.at[layer, k, t]))
+            else:
+                out.append(pltpu.make_async_copy(here, dst.at[layer, rows], q_out.at[layer, k, t]))
+        return out
+
+    def start(cps):
+        for cp in cps:
+            cp.start()
+
+    def wait(cps):
+        for cp in cps:
+            cp.wait()
 
     x_cp = pltpu.make_async_copy(x_hbm, xb, g_sem.at[CH])
     g_cps = [pltpu.make_async_copy(g_hbm.at[i], g_all.at[i], g_sem.at[i]) for i in range(CH)]
     gv1_cp = pltpu.make_async_copy(gv1_hbm, gv1, g_sem.at[CH + 1])
     gh_cp = pltpu.make_async_copy(gh_hbm, gh, g_sem.at[CH + 2])
-    x_cp.start()
-    g_cps[CH - 1].start()
-    for cp in ins[:4]:
-        cp.start()
-
-    def update(w, v, g, scale):
-        nv = MOMENTUM * v + scale * g.astype(F32)
-        nw = w - nv
-        return nw, nv
-
-    x_cp.wait()
-    g_cps[CH - 1].wait()
-    for cp in ins[:4]:
-        cp.wait()
-    for i in (4, 5, 2, 3):
-        g_cps[i].start()
-    for t in QUADS:
-        for k in QUADS:
-            qin(0, t, k).start()
-    ins[4].start()
-    ins[5].start()
-    g_cps[0].start()
-    g_cps[1].start()
-    gv1_cp.start()
-    gh_cp.start()
-    ins[6].start()
-    ins[7].start()
-    for b in PAIR:
-        nw, nv = update(suo[b], tuo[b], gsm[D1 * b:D1 * (b + 1), :], scal[b:b + 1, 0:1])
-        suo[b] = nw
-        tuo[b] = nv
-        wuo[b] = nw.astype(BF16)
-        for q in PAIR:
-            rows = slice(TILE * q, TILE * (q + 1))
-            nw, nv = update(sdo[b, rows, :], tdo[b, rows, :], gsm[TILE:D2, TILE * b + D1 * q:TILE * b + D1 * (q + 1)], scal[2 + b:3 + b, 0:1])
-            sdo[b, rows, :] = nw
-            tdo[b, rows, :] = nv
-            wdo[b, rows, :] = nw.astype(BF16)
-    for cp in louts[:4]:
-        cp.start()
-
-    def loop_update(wbuf, vbuf, gref, wdst, base, count, scale, gbase):
-        def body(i, carry):
-            rows = ds(base + i * MT, MT)
-            nw, nv = update(wbuf[rows, :], vbuf[rows, :], gref[ds(gbase + i * MT, MT), :], scale)
-            wbuf[rows, :] = nw
-            vbuf[rows, :] = nv
-            wdst[rows, :] = nw.astype(BF16)
-            return carry
-
-        lax.fori_loop(0, count // MT, body, 0)
-
-    def big_update(layer, t):
-        for k in QUADS:
-            qin(layer, t, k).wait()
-        up_scale, down_scale = scal[4 + layer:5 + layer, 0:1], scal[6 + layer:7 + layer, 0:1]
-
-        def up_body(i, carry):
-            rows = ds(t * D1 + i * IMAGES, IMAGES)
-            for q in QUADS:
-                cols = slice(D2 * q, D2 * (q + 1))
-                g = g_all[4 - 4 * layer + q // 2, ds((q % 2) * D2 + t * D1 + i * IMAGES, IMAGES), :]
-                nw, nv = update(sut[rows, cols], tut[rows, cols], g, up_scale)
-                sut[rows, cols] = nw
-                tut[rows, cols] = nv
-                wut[layer, rows, cols] = nw.astype(BF16)
-            return carry
-
-        lax.fori_loop(0, D1 // IMAGES, up_body, 0)
-        if layer == 0:
-            loop_update(sdt, tdt, g_all.at[2 + t // 2], wdt.at[0], t * D2, D2, down_scale, (t % 2) * D2)
-        else:
-            loop_update(sdt, tdt, gv1, wdt.at[1], t * D2, D2, down_scale, t * D2)
-        for k in QUADS:
-            qout(layer, t, k).start()
-
-    def refill(t):
-        for k in QUADS:
-            qout(0, t, k).wait()
-        for k in QUADS:
-            qin(1, t, k).start()
-
-    def stage_one(t, carry):
-        xf[...] = xb[ds(t * ROWS2, ROWS2), :].astype(F32)
-        r = jnp.concatenate([xf[pl.ds(j, TILE, stride=4), :] for j in QUADS], axis=0)
-        for b in PAIR:
-            xhat, _ = ln_parts(r)
-            a = gelu_only(nn(xhat.astype(BF16), wuo[b])).astype(BF16)
-            rb = (r + nn(a, wdo[b])).astype(BF16)
-            r = rb.astype(F32)
-        for j in QUADS:
-            r2[ds(t * TILE, TILE), D1 * j:D1 * (j + 1)] = rb[TILE * j:TILE * (j + 1), :]
-
-        @pl.when(t == 0)
-        def _():
-            for i in (4, 5, 2, 3):
-                g_cps[i].wait()
-
-        big_update(0, t)
-
-        @pl.when(t > 0)
-        def _():
-            refill(t - 1)
-
-        return carry
-
-    lax.fori_loop(0, NTILE, stage_one, 0)
-    for cp in ins[4:6]:
-        cp.wait()
-    loop_update(sm, tm, gsm.at[D2:ROWS2], wm, 0, D2, scal[SUB:9, 0:1], 0)
-    for cp in louts[4:6]:
-        cp.start()
-    refill(3)
-    g_cps[0].wait()
-    g_cps[1].wait()
-    gv1_cp.wait()
-    pooled[...] = jnp.zeros_like(pooled)
+
+    def up_part(layer, t):
+        scale = scal[4 + layer:5 + layer, 0:1]
+        rows = ds(t * D1, D1)
+        for q in QUADS:
+            cols = slice(D2 * q, D2 * (q + 1))
+            g = g_all[4 - 4 * layer + q // 2, ds((q % 2) * D2 + t * D1, D1), :]
+            nw, nv = update(sut[rows, cols], tut[rows, cols], g, scale)
+            sut[rows, cols] = nw
+            tut[rows, cols] = nv
+            wut[layer, rows, cols] = nw.astype(BF16)
+
+    def down_part(layer, t):
+        rows = ds(t * D2, D2)
+        g = g_all[2 + t // 2, ds((t % 2) * D2, D2), :] if layer == 0 else gv1[rows, :]
+        nw, nv = update(sdt[layer, rows, :], tdt[layer, rows, :], g, scal[6 + layer:7 + layer, 0:1])
+        sdt[layer, rows, :] = nw
+        tdt[layer, rows, :] = nv
+        wdt[layer, rows, :] = nw.astype(BF16)
 
     def stage_two(layer, r):
         xhat, _ = ln_parts(r)
@@ -780,32 +713,110 @@
             acc = acc + nn(a, wdt[layer, cols, :])
         return acc.astype(BF16)
 
+    first_in = [x_cp, g_cps[CH - 1]] + ins[:4]
+    early = [g_cps[i] for i in (4, 5, 2)]
+    later = [g_cps[0], g_cps[1], gv1_cp]
+    start(first_in)
+    start(early)
+    start(copies(0, 0, True))
+    wait(first_in)
+    for b in PAIR:
+        nw, tuo[b] = update(suo[b], tuo[b], gsm[D1 * b:D1 * (b + 1), :], scal[b:b + 1, 0:1])
+        suo[b] = nw
+        wuo[b] = nw.astype(BF16)
+        for q in PAIR:
+            rows = slice(TILE * q, TILE * (q + 1))
+            nw, tdo[b, rows, :] = update(sdo[b, rows, :], tdo[b, rows, :], gsm[TILE:D2, TILE * b + D1 * q:TILE * b + D1 * (q + 1)], scal[2 + b:3 + b, 0:1])
+            sdo[b, rows, :] = nw
+            wdo[b, rows, :] = nw.astype(BF16)
+    wait(early)
+
+    def stage_one_update(t, carry):
+        wait(copies(0, t, True))
+
+        @pl.when(t < 3)
+        def _():
+            start(copies(0, t + 1, True))
+
+        @pl.when(t == 0)
+        def _():
+            start([g_cps[3]])
+
+        @pl.when(t == 1)
+        def _():
+            start(ins[4:6])
+
+        @pl.when(t == 2)
+        def _():
+            wait([g_cps[3]])
+            start(later)
+
+        @pl.when(t == 3)
+        def _():
+            start(copies(1, 0, True, DOWNS))
+            start(copies(1, 1, True, DOWNS))
+            start([gh_cp] + ins[6:])
+
+        stage_one_tile(t, xb, xf, wuo, wdo, r2)
+        up_part(0, t)
+        down_part(0, t)
+        start(copies(0, t, False, PAIR))
+        return carry
+
+    lax.fori_loop(0, NTILE, stage_one_update, 0)
+    start(copies(1, 2, True, DOWNS))
+    start(copies(1, 3, True, DOWNS))
+    wait(ins[4:6])
+    nw, tm[...] = update(sm[...], tm[...], gsm[D2:ROWS2, :], scal[SUB:9, 0:1])
+    sm[...] = nw
+    wm[...] = nw.astype(BF16)
+
+    def merge_tile(t, carry):
+        rows = ds(t * WIDE, WIDE)
+        r2[rows, :] = nn(r2[rows, :], wm[...]).astype(BF16)
+        return carry
+
+    lax.fori_loop(0, ROWS2 // WIDE, merge_tile, 0)
+    wait(later)
+    pooled[...] = jnp.zeros_like(pooled)
+
     def first(t, carry):
         rows = ds(t * WIDE, WIDE)
-        r = nn(r2[rows, :], wm[...]).astype(BF16).astype(F32)
-        r2[rows, :] = stage_two(0, r)
-
-        def both(i, inner):
-            big_update(1, 2 * t + i)
-            return inner
-
-        lax.fori_loop(0, 2, both, 0)
+        for i in PAIR:
+            wait(copies(0, 2 * t + i, False, PAIR))
+            start(copies(1, 2 * t + i, True, PAIR))
+        for i in PAIR:
+            wait(copies(1, 2 * t + i, True, DOWNS))
+            start(copies(0, 2 * t + i, False, DOWNS))
+        r2[rows, :] = stage_two(0, r2[rows, :].astype(F32))
+        for i in PAIR:
+            down_part(1, 2 * t + i)
         return carry
 
     lax.fori_loop(0, ROWS2 // WIDE, first, 0)
-
+    def second_up(t, carry):
+        wait(copies(1, t, True, PAIR))
+        up_part(1, t)
+        start(copies(1, t, False))
+        return carry
+
+    lax.fori_loop(0, NTILE, second_up, 0)
+    start(louts[:6])
     wh[CLASSES:, :] = jnp.zeros((CPAD - CLASSES, D2), BF16)
-    ins[6].wait()
-    ins[7].wait()
-    gh_cp.wait()
-    for k in QUADS:
-        rows = slice(TILE * k, min(TILE * (k + 1), CLASSES))
-        nw, nv = update(sh[rows, :], th[rows, :], gh[rows, :], scal[9:10, 0:1])
+    wait(ins[6:] + [gh_cp])
+
+    def head_update(rows):
+        nw, th[rows, :] = update(sh[rows, :], th[rows, :], gh[rows, :], scal[9:10, 0:1])
         sh[rows, :] = nw
-        th[rows, :] = nv
         wh[rows, :] = nw.astype(BF16)
-    for cp in louts[6:]:
-        cp.start()
+
+    def head_part(i, carry):
+        head_update(ds(i * HEAD_STEP, HEAD_STEP))
+        return carry
+
+    lax.fori_loop(0, CLASSES // HEAD_STEP, head_part, 0)
+    head_update(slice(CLASSES - CLASSES % HEAD_STEP, CLASSES))
+    start(louts[6:])
 
     def second(t, carry):
         rows = ds(t * WIDE, WIDE)
@@ -817,11 +828,10 @@
     xhat, _ = ln_parts(pooled[...] * (1.0 / MT))
     logits = nt(xhat.astype(BF16), wh[...])
     logits_out[...] = logits[:, 0:CLASSES]
-    for cp in louts:
-        cp.wait()
+    wait(louts)
     for t in QUADS:
-        for k in QUADS:
-            qout(1, t, k).wait()
+        wait(copies(0, t, False, DOWNS))
+        wait(copies(1, t, False))
 
 
 def weight_scratch():
@@ -829,7 +839,7 @@
 
 
 def master_scratch():
-    return [pltpu.VMEM((2, D1, H1), F32), pltpu.VMEM((2, H1, D1), F32), pltpu.VMEM((D2, D2), F32), pltpu.VMEM((CLASSES, D2), F32), pltpu.VMEM((D2, H2), F32), pltpu.VMEM((H2, D2), F32)]
+    return [pltpu.VMEM((2, D1, H1), F32), pltpu.VMEM((2, H1, D1), F32), pltpu.VMEM((D2, D2), F32), pltpu.VMEM((CLASSES, D2), F32), pltpu.VMEM((D2, H2), F32), pltpu.VMEM((2, H2, D2), F32)]
 
 
 def solution(mesh):
@@ -847,7 +857,7 @@
         in_specs=[hbm, smem] + [hbm] * 6,
         out_specs=[hbm] * 3 + [vmem],
         scratch_shapes=[pltpu.VMEM((CH, ROWS2 // k, D2), BF16) for k in (1, 2, 4, NDEV)]
-        + [pltpu.VMEM((NDEV, 32, LRW), BF16)]
+        + [pltpu.VMEM((NDEV, 32, LRW), BF16), pltpu.VMEM((NDEV, 32, D2), BF16)]
         + weight_scratch()
         + [pltpu.VMEM((ROWS2, D2), BF16), pltpu.VMEM((2, ROWS1, D1), BF16), pltpu.VMEM((ROWS1, 1), F32), pltpu.VMEM((ROWS2, D2), BF16), pltpu.VMEM((2, ROWS2, D2), BF16), pltpu.VMEM((2, ROWS2, 1), F32), pltpu.VMEM((ROWS2, H2), BF16), pltpu.VMEM((2, ROWS2, H2), BF16), pltpu.VMEM((IMAGES, D2), F32), pltpu.VMEM((IMAGES, H2), F32), pltpu.VMEM((2, H1, D1), F32), pltpu.VMEM((2, D1, H1), F32), pltpu.VMEM((10, SUB, D1), F32), pltpu.VMEM((10, SUB, D1), F32)]
         + [dma((5,)), dma((2,)), dma((CH + 2,)), dma((CH, 10)), dma((CH, 10)), pltpu.SemaphoreType.REGULAR((CH, 3)), dma((CH,)), dma((CH,))],
@@ -865,7 +875,7 @@
         + master_scratch() * 2
         + weight_scratch()
         + [pltpu.VMEM((ROWS2, D2), BF16), pltpu.VMEM((IMAGES, D2), F32)]
-        + [dma((SUB,)), dma((SUB,)), dma((4, 4)), dma((4, 4)), dma((CH + 3,))],
+        + [dma((SUB,)), dma((SUB,)), dma((2, 4, 4)), dma((2, 4, 4)), dma((CH + 3,))],
         compiler_params=pltpu.CompilerParams(vmem_limit_bytes=VMEM_LIMIT),
         name="step",
     )

time: 158 us -> 149 us (0.943)
  Pallas kernels: 157 us -> 148 us
    pallas_call x1, Pallas kernels: 117 us -> 110 us  [local_step(): got = grads_call(x_now.reshape(ROWS1, D1), labels_now, *params)]
    pallas_call x1, Pallas kernels: 40.6 us -> 37.7 us  [local_step(): outs = list(step_call(x_next.reshape(ROWS1, D1), *params, *vels, *got))]
where the time goes in v1:
time: 149 us
  Pallas kernels  148 us (99%)
    pallas_call x1, Pallas kernels, local_step(): got = grads_call(x_now.reshape(ROWS1, D1), labels_now, *params)  110 us
    pallas_call x1, Pallas kernels, local_step(): outs = list(step_call(x_next.reshape(ROWS1, D1), *params, *vels, *got))  37.7 us

profile of v1, /device:TPU:0, one launch (start us, length us, event | category | flops | bytes accessed | tf_op | source)
XLA Modules:
  0.0 149.0 jit_solution(749517175838968484)
XLA Ops:
  0.6 110.5 %grads.1 = (bf16[7,1024,512]{2,1,0:T(8,128)(2,1)}, bf16[2048,512]{1,0:T(8,128)(2,1)}, bf16[1024,512]{1,0:T(8,128)(2,1)}, f32[16,128]{1,0:T(8,128)}) custom-call(bf16[4096,128]{1,0:T(8,128)(2,1)} %bitcast.9, s32[16]{0:T(128)} %lab.1, f32[2,128,512]{2,1,0:T(8,128)} %uo_hbm.3, f32[2,512,128]{2,1,0:T(8,128)} %do_hbm.3, f32[512,512]{1,0:T(8,128)} %m_hbm.3, ...), custom_call_target="tpu_custom_call" | custom-call | tf_op jit(solution)/shard_map/grads/pallas_call | solution.py:886
  111.1 37.7 %step.1 = (f32[16,1000]{1,0:T(8,128)}, f32[2,128,512]{2,1,0:T(8,128)}, f32[2,512,128]{2,1,0:T(8,128)}, f32[512,512]{1,0:T(8,128)}, f32[2,512,2048]{2,1,0:T(8,128...) custom-call(bf16[4096,128]{1,0:T(8,128)(2,1)} %bitcast.10, ...), custom_call_target="tpu_custom_call" | custom-call | tf_op jit(solution)/shard_map/step/pallas_call | solution.py:887

commit v2 on v1

--- a/solution.py
+++ b/solution.py
@@ -30,7 +30,7 @@
 WIDE = 512
 HEAD_STEP = 192
 CH = 7
-LETTERS = 'abcdefg'
+LETTERS = 'abcdefgh'
 NORM_ROW = dict(a=5, b=5, c=6, d=6, e=4, f=4)
 LRW = 3072
 LRG = 2560
@@ -127,13 +127,21 @@
     return nw, nv
 
 
+def chunk_of(num, ref):
+    if num < CH - 1:
+        return ref.at[num]
+    half = ref.shape[1] // 2
+    return ref.at[CH - 1, pl.ds((num - CH + 1) * half, half)]
+
+
 class Ring:
-    def __init__(self, num, g, r1, r2, r3, ssem, rsem, csem, pos):
+    def __init__(self, num, stacks, ssem, rsem, csem, pos):
         self.num = num
-        self.g, self.r1, self.r2, self.r3 = (ref.at[num] for ref in (g, r1, r2, r3))
+        self.g, self.r1, self.r2, self.r3 = (chunk_of(num, ref) for ref in stacks)
+        g = self.g
         self.ssem, self.rsem, self.csem = ssem, rsem, csem
         self.pos = pos
-        self.rb = g.shape[1] // NDEV
+        self.rb = g.shape[0] // NDEV
         c, f, s = pos['c'], pos['f'], pos['s']
         self.f, self.s, self.nf, self.ns = f, s, 1 - f, 1 - s
         self.mine, self.other = 4 * c, 4 - 4 * c
@@ -304,16 +312,16 @@
 SHARE_STEPS = ('send', 'relay', 'done')
 PLAN = dict(
     up1=((), ('a0',), (), ('b0',),),
-    in1=(('a1',), ('s1',), ('b1',), (),),
+    in1=((), ('a1',), ('s1', 'b1',), (),),
     dn0=((), ('c0',), (), ('d0',),),
-    pre0=(('a2', 'c1', 's2',), ('d1',), (), ('b2',),),
-    up0=((), ('a3', 'e0',), (), ('a4', 'f0',),),
-    in0=(('e1', 'c2', 'b3',), ('f1', 'b4',), (), ('a5',),),
-    mrg=((),),
-    back=(('a6', 'c3', 'd2',), ('b5', 'c4', 'e2',), ('b6', 'd3',), ('c5', 'd4', 'e3', 'a7', 'f2', 'g0',),),
-    rank=(('c6', 'a8', 'e4',), ('g1', 'b7',), ('d5',), ('b8', 'd6',),),
-    rankh=((), ('f3',), (), ('c7', 'f4',),),
-    tail=('e5', 'e6', 'c8', 'f5', 'g2', 'd7', 'd8', 'f6', 'g3', 'e7', 'g4', 'f7', 'e8', 'f8', 'g5', 'g6', 'g7', 'g8', ),
+    pre0=((), ('c1', 'a2',), ('s2', 'd1',), (),),
+    up0=((), ('b2', 'e0',), (), ('f0',),),
+    in0=(('a3', 'e1',), ('a4', 'c2', 'f1',), ('b3',), (),),
+    mrg=(('b4', 'h0',),),
+    back=(('a5', 'a6', 'd2', 'h1',), ('b5', 'c3',), ('c4', 'd3', 'e2', 'f2',), ('a7', 'b6', 'd4', 'g0',),),
+    rank=(('c5', 'h2',), ('a8', 'g1',), ('b7', 'e3',), ('e4',),),
+    rankh=(('b8', 'c6', 'f3',), (), ('f4',), ('d5',),),
+    tail=('d6', 'h3', 'h4', 'c7', 'e5', 'c8', 'g2', 'f5', 'h5', 'e6', 'g3', 'f6', 'g4', 'd7', 'h6', 'd8', 'e7', 'g5', 'f7', 'e8', 'h7', 'g6', 'f8', 'g7', 'h8', 'g8', ),
 )
 
 
@@ -331,8 +339,8 @@
     gv1, gh, grad = wdt.at[1], wh, r2
 
     share = Share(lr, lssem, lrsem, pos)
-    rings = {letter: Ring(i, g_all, r1_all, r2_all, r3_all, ssem, rsem, csem, pos) for i, letter in enumerate(LETTERS)}
-    outs = {letter: pltpu.make_async_copy(g_all.at[i], g_out.at[i], out_sem.at[i]) for i, letter in enumerate(LETTERS)}
+    rings = {letter: Ring(i, (g_all, r1_all, r2_all, r3_all), ssem, rsem, csem, pos) for i, letter in enumerate(LETTERS)}
+    outs = {letter: pltpu.make_async_copy(chunk_of(i, g_all), chunk_of(i, g_out), out_sem.at[i]) for i, letter in enumerate(LETTERS)}
 
     def norm_of(letter):
         ref = g_all.at[LETTERS.index(letter)]
@@ -620,8 +628,8 @@
         gh[rows, :] = ob
         gsq[9] += fold_sq(ob.astype(F32))
 
-    gv1_cp = pltpu.make_async_copy(gv1, gv1_out, out_sem.at[CH])
-    gh_cp = pltpu.make_async_copy(gh, gh_out, out_sem.at[CH + 1])
+    gv1_cp = pltpu.make_async_copy(gv1, gv1_out, out_sem.at[CH + 1])
+    gh_cp = pltpu.make_async_copy(gh, gh_out, out_sem.at[CH + 2])
     for d in range(NDEV):
         gdup[d, 0:IMAGES, :] = lr[d, 0:IMAGES, H2:LRG]
         gdup[d, IMAGES:32, :] = lr[d, 0:IMAGES, H2:LRG]
@@ -860,7 +868,7 @@
         + [pltpu.VMEM((NDEV, 32, LRW), BF16), pltpu.VMEM((NDEV, 32, D2), BF16)]
         + weight_scratch()
         + [pltpu.VMEM((ROWS2, D2), BF16), pltpu.VMEM((2, ROWS1, D1), BF16), pltpu.VMEM((ROWS1, 1), F32), pltpu.VMEM((ROWS2, D2), BF16), pltpu.VMEM((2, ROWS2, D2), BF16), pltpu.VMEM((2, ROWS2, 1), F32), pltpu.VMEM((ROWS2, H2), BF16), pltpu.VMEM((2, ROWS2, H2), BF16), pltpu.VMEM((IMAGES, D2), F32), pltpu.VMEM((IMAGES, H2), F32), pltpu.VMEM((2, H1, D1), F32), pltpu.VMEM((2, D1, H1), F32), pltpu.VMEM((10, SUB, D1), F32), pltpu.VMEM((10, SUB, D1), F32)]
-        + [dma((5,)), dma((2,)), dma((CH + 2,)), dma((CH, 10)), dma((CH, 10)), pltpu.SemaphoreType.REGULAR((CH, 3)), dma((CH,)), dma((CH,))],
+        + [dma((5,)), dma((2,)), dma((CH + 3,)), dma((CH + 1, 10)), dma((CH + 1, 10)), pltpu.SemaphoreType.REGULAR((CH + 1, 3)), dma((CH,)), dma((CH,))],
         compiler_params=pltpu.CompilerParams(collective_id=0, has_side_effects=True, vmem_limit_bytes=VMEM_LIMIT),
         name="grads",
     )

time: 149 us -> 147 us (0.987)
  Pallas kernels: 148 us -> 146 us
    pallas_call x1, Pallas kernels: 110 us -> 109 us  [local_step(): got = grads_call(x_now.reshape(ROWS1, D1), labels_now, *params)]
where the time goes in v2:
time: 147 us
  Pallas kernels  146 us (99%)
    pallas_call x1, Pallas kernels, local_step(): got = grads_call(x_now.reshape(ROWS1, D1), labels_now, *params)  109 us
    pallas_call x1, Pallas kernels, local_step(): outs = list(step_call(x_next.reshape(ROWS1, D1), *params, *vels, *got))  37.7 us

profile of v2, /device:TPU:0, one launch (start us, length us, event | category | flops | bytes accessed | tf_op | source)
XLA Modules:
  0.0 147.2 jit_solution(14391199487751572041)
XLA Ops:
  0.6 108.7 %grads.1 = (bf16[7,1024,512]{2,1,0:T(8,128)(2,1)}, bf16[2048,512]{1,0:T(8,128)(2,1)}, bf16[1024,512]{1,0:T(8,128)(2,1)}, f32[16,128]{1,0:T(8,128)}) custom-call(bf16[4096,128]{1,0:T(8,128)(2,1)} %bitcast.9, s32[16]{0:T(128)} %lab.1, f32[2,128,512]{2,1,0:T(8,128)} %uo_hbm.3, f32[2,512,128]{2,1,0:T(8,128)} %do_hbm.3, f32[512,512]{1,0:T(8,128)} %m_hbm.3, ...), custom_call_target="tpu_custom_call" | custom-call | tf_op jit(solution)/shard_map/grads/pallas_call | solution.py:894
  109.4 37.7 %step.1 = (f32[16,1000]{1,0:T(8,128)}, f32[2,128,512]{2,1,0:T(8,128)}, f32[2,512,128]{2,1,0:T(8,128)}, f32[512,512]{1,0:T(8,128)}, f32[2,512,2048]{2,1,0:T(8,128...) custom-call(bf16[4096,128]{1,0:T(8,128)(2,1)} %bitcast.10, ...), custom_call_target="tpu_custom_call" | custom-call | tf_op jit(solution)/shard_map/step/pallas_call | solution.py:895

commit v3 on v2

--- a/solution.py
+++ b/solution.py
@@ -13,7 +13,7 @@
 MESH = pl.DeviceIdType.MESH
 F32 = jnp.float32
 BF16 = jnp.bfloat16
-VMEM_LIMIT = 67043328
+SCOPED_LIMIT = 59600000
 
 IMAGES = 16
 TOKENS = 256
@@ -326,8 +326,8 @@
 
 
 def grad_kernel(x_hbm, lab, uo_hbm, do_hbm, m_hbm, ut_hbm, dt_hbm, h_hbm,
-                g_out, gv1_out, gh_out, scal,
-                g_all, r1_all, r2_all, r3_all, lr, gdup,
+                g_all, gv1_out, gh_out, scal,
+                r1_all, r2_all, r3_all, lr, gdup,
                 wuo, wdo, wm, wut, wdt, wh,
                 merged, n1, rst1, r2, n2, rst2, a2, sl2, pooled, asum, accv, accu, sq, gsq,
                 in_sem, st_sem, out_sem, ssem, rsem, csem, lssem, lrsem):
@@ -340,7 +340,6 @@
 
     share = Share(lr, lssem, lrsem, pos)
     rings = {letter: Ring(i, (g_all, r1_all, r2_all, r3_all), ssem, rsem, csem, pos) for i, letter in enumerate(LETTERS)}
-    outs = {letter: pltpu.make_async_copy(chunk_of(i, g_all), chunk_of(i, g_out), out_sem.at[i]) for i, letter in enumerate(LETTERS)}
 
     def norm_of(letter):
         ref = g_all.at[LETTERS.index(letter)]
@@ -357,7 +356,6 @@
         else:
             getattr(rings[letter], STEPS[num])()
             if STEPS[num] == 'done':
-                outs[letter].start()
                 if letter in NORM_ROW:
                     norm_of(letter)
 
@@ -628,8 +626,8 @@
         gh[rows, :] = ob
         gsq[9] += fold_sq(ob.astype(F32))
 
-    gv1_cp = pltpu.make_async_copy(gv1, gv1_out, out_sem.at[CH + 1])
-    gh_cp = pltpu.make_async_copy(gh, gh_out, out_sem.at[CH + 2])
+    gv1_cp = pltpu.make_async_copy(gv1, gv1_out, out_sem.at[0])
+    gh_cp = pltpu.make_async_copy(gh, gh_out, out_sem.at[1])
     for d in range(NDEV):
         gdup[d, 0:IMAGES, :] = lr[d, 0:IMAGES, H2:LRG]
         gdup[d, IMAGES:32, :] = lr[d, 0:IMAGES, H2:LRG]
@@ -647,16 +645,14 @@
         ratio = jnp.sqrt(total(sq[i])) / jnp.sqrt(total(gsq[i]))
         scal[i:i + 1, :] = jnp.broadcast_to(TRUST * ratio, (1, D1))
     scal[10:IMAGES, :] = jnp.zeros((6, D1), F32)
-    for letter in LETTERS:
-        outs[letter].wait()
     gv1_cp.wait()
     gh_cp.wait()
 
 
 def step_kernel(x_hbm, uo_hbm, do_hbm, m_hbm, ut_hbm, dt_hbm, h_hbm, vuo_hbm, vdo_hbm, vm_hbm, vut_hbm, vdt_hbm, vh_hbm,
-                g_hbm, gv1_hbm, gh_hbm, scal,
+                g_all, gv1_hbm, gh_hbm, scal,
                 logits_out, uo_out, do_out, m_out, ut_out, dt_out, h_out, vuo_out, vdo_out, vm_out, vut_out, vdt_out, vh_out,
-                xb, xf, g_all, gv1, gh, suo, sdo, sm, sh, sut, sdt, tuo, tdo, tm, th, tut, tdt,
+                xb, xf, gv1, gh, suo, sdo, sm, sh, sut, sdt, tuo, tdo, tm, th, tut, tdt,
                 wuo, wdo, wm, wut, wdt, wh, r2, pooled,
                 s_in, s_out, q_in, q_out, g_sem):
     small = [(uo_hbm, suo, uo_out), (vuo_hbm, tuo, vuo_out), (do_hbm, sdo, do_out), (vdo_hbm, tdo, vdo_out), (m_hbm, sm, m_out), (vm_hbm, tm, vm_out), (h_hbm, sh, h_out), (vh_hbm, th, vh_out)]
@@ -688,7 +684,6 @@
             cp.wait()
 
     x_cp = pltpu.make_async_copy(x_hbm, xb, g_sem.at[CH])
-    g_cps = [pltpu.make_async_copy(g_hbm.at[i], g_all.at[i], g_sem.at[i]) for i in range(CH)]
     gv1_cp = pltpu.make_async_copy(gv1_hbm, gv1, g_sem.at[CH + 1])
     gh_cp = pltpu.make_async_copy(gh_hbm, gh, g_sem.at[CH + 2])
 
@@ -721,11 +716,9 @@
             acc = acc + nn(a, wdt[layer, cols, :])
         return acc.astype(BF16)
 
-    first_in = [x_cp, g_cps[CH - 1]] + ins[:4]
-    early = [g_cps[i] for i in (4, 5, 2)]
-    later = [g_cps[0], g_cps[1], gv1_cp]
+    first_in = [x_cp] + ins[:4]
+    later = [gv1_cp]
     start(first_in)
-    start(early)
     start(copies(0, 0, True))
     wait(first_in)
     for b in PAIR:
@@ -737,7 +730,6 @@
             nw, tdo[b, rows, :] = update(sdo[b, rows, :], tdo[b, rows, :], gsm[TILE:D2, TILE * b + D1 * q:TILE * b + D1 * (q + 1)], scal[2 + b:3 + b, 0:1])
             sdo[b, rows, :] = nw
             wdo[b, rows, :] = nw.astype(BF16)
-    wait(early)
 
     def stage_one_update(t, carry):
         wait(copies(0, t, True))
@@ -746,17 +738,12 @@
         def _():
             start(copies(0, t + 1, True))
 
-        @pl.when(t == 0)
-        def _():
-            start([g_cps[3]])
-
         @pl.when(t == 1)
         def _():
             start(ins[4:6])
 
         @pl.when(t == 2)
         def _():
-            wait([g_cps[3]])
             start(later)
 
         @pl.when(t == 3)
@@ -861,30 +848,30 @@
 
     grads_call = pl.pallas_call(
         grad_kernel,
-        out_shape=wide_g + [shape((IMAGES, D1), F32)],
+        out_shape=[pltpu.VMEM(wide_g[0].shape, BF16)] + wide_g[1:] + [shape((IMAGES, D1), F32)],
         in_specs=[hbm, smem] + [hbm] * 6,
-        out_specs=[hbm] * 3 + [vmem],
-        scratch_shapes=[pltpu.VMEM((CH, ROWS2 // k, D2), BF16) for k in (1, 2, 4, NDEV)]
+        out_specs=[vmem] + [hbm] * 2 + [vmem],
+        scratch_shapes=[pltpu.VMEM((CH, ROWS2 // k, D2), BF16) for k in (2, 4, NDEV)]
         + [pltpu.VMEM((NDEV, 32, LRW), BF16), pltpu.VMEM((NDEV, 32, D2), BF16)]
         + weight_scratch()
         + [pltpu.VMEM((ROWS2, D2), BF16), pltpu.VMEM((2, ROWS1, D1), BF16), pltpu.VMEM((ROWS1, 1), F32), pltpu.VMEM((ROWS2, D2), BF16), pltpu.VMEM((2, ROWS2, D2), BF16), pltpu.VMEM((2, ROWS2, 1), F32), pltpu.VMEM((ROWS2, H2), BF16), pltpu.VMEM((2, ROWS2, H2), BF16), pltpu.VMEM((IMAGES, D2), F32), pltpu.VMEM((IMAGES, H2), F32), pltpu.VMEM((2, H1, D1), F32), pltpu.VMEM((2, D1, H1), F32), pltpu.VMEM((10, SUB, D1), F32), pltpu.VMEM((10, SUB, D1), F32)]
-        + [dma((5,)), dma((2,)), dma((CH + 3,)), dma((CH + 1, 10)), dma((CH + 1, 10)), pltpu.SemaphoreType.REGULAR((CH + 1, 3)), dma((CH,)), dma((CH,))],
-        compiler_params=pltpu.CompilerParams(collective_id=0, has_side_effects=True, vmem_limit_bytes=VMEM_LIMIT),
+        + [dma((5,)), dma((2,)), dma((2,)), dma((CH + 1, 10)), dma((CH + 1, 10)), pltpu.SemaphoreType.REGULAR((CH + 1, 3)), dma((CH,)), dma((CH,))],
+        compiler_params=pltpu.CompilerParams(collective_id=0, has_side_effects=True, vmem_limit_bytes=SCOPED_LIMIT),
         name="grads",
     )
 
     step_call = pl.pallas_call(
         step_kernel,
         out_shape=[shape((IMAGES, CLASSES), F32)] + masters * 2,
-        in_specs=[hbm] * 16 + [vmem],
+        in_specs=[hbm] * 13 + [vmem] + [hbm] * 2 + [vmem],
         out_specs=[vmem] + [hbm] * 12,
         scratch_shapes=[pltpu.VMEM((ROWS1, D1), BF16), pltpu.VMEM((ROWS2, D1), F32)]
-        + [pltpu.VMEM(g.shape, BF16) for g in wide_g]
+        + [pltpu.VMEM(g.shape, BF16) for g in wide_g[1:]]
         + master_scratch() * 2
         + weight_scratch()
         + [pltpu.VMEM((ROWS2, D2), BF16), pltpu.VMEM((IMAGES, D2), F32)]
         + [dma((SUB,)), dma((SUB,)), dma((2, 4, 4)), dma((2, 4, 4)), dma((CH + 3,))],
-        compiler_params=pltpu.CompilerParams(vmem_limit_bytes=VMEM_LIMIT),
+        compiler_params=pltpu.CompilerParams(vmem_limit_bytes=SCOPED_LIMIT),
         name="step",
     )
 
@@ -892,7 +879,8 @@
         params = (up_one, down_one, merge_proj, up_two, down_two, head_proj.T)
         vels = (vel_up_one, vel_down_one, vel_merge_proj, vel_up_two, vel_down_two, vel_head_proj.T)
         got = grads_call(x_now.reshape(ROWS1, D1), labels_now, *params)
-        outs = list(step_call(x_next.reshape(ROWS1, D1), *params, *vels, *got))
+        stack = pltpu.with_memory_space_constraint(got[0], pltpu.VMEM)
+        outs = list(step_call(x_next.reshape(ROWS1, D1), *params, *vels, stack, *got[1:]))
         outs[6], outs[12] = outs[6].T, outs[12].T
         return tuple(outs)
 

time: 147 us -> 146 us (level)
  no operation moved by 1% of the time
where the time goes in v3:
time: 146 us
  Pallas kernels  145 us (99%)
    pallas_call x1, Pallas kernels, local_step(): got = grads_call(x_now.reshape(ROWS1, D1), labels_now, *params)  108 us
    pallas_call x1, Pallas kernels, local_step(): step_call(x_next.reshape(ROWS1, D1), *params, *vels, stack, *got[1:])  37 us

profile of v3, /device:TPU:0, one launch (start us, length us, event | category | flops | bytes accessed | tf_op | source)
XLA Modules:
  0.0 145.8 jit_solution(123503802519672731)
XLA Ops:
  0.6 108.0 %grads.1 = (bf16[7,1024,512]{2,1,0:T(8,128)(2,1)S(1)}, bf16[2048,512]{1,0:T(8,128)(2,1)}, bf16[1024,512]{1,0:T(8,128)(2,1)}, f32[16,128]{1,0:T(8,128)}) custom-call(bf16[4096,128]{1,0:T(8,128)(2,1)} %bitcast.9, s32[16]{0:T(128)} %lab.1, f32[2,128,512]{2,1,0:T(8,128)} %uo_hbm.3, f32[2,512,128]{2,1,0:T(8,128)} %do_hbm.3, f32[512,512]{1,0:T(8,128)} %m_hbm.3, ...), custom_call_target="tpu_custom_call" | custom-call | tf_op jit(solution)/shard_map/grads/pallas_call | solution.py:881
  108.7 37.0 %step.1 = (f32[16,1000]{1,0:T(8,128)}, f32[2,128,512]{2,1,0:T(8,128)}, f32[2,512,128]{2,1,0:T(8,128)}, f32[512,512]{1,0:T(8,128)}, f32[2,512,2048]{2,1,0:T(8,128...) custom-call(bf16[4096,128]{1,0:T(8,128)(2,1)} %bitcast.10, ...), custom_call_target="tpu_custom_call" | custom-call | tf_op jit(solution)/shard_map/step/pallas_call | solution.py:883

commit v4 on v3

--- a/solution.py
+++ b/solution.py
@@ -741,15 +741,16 @@
         @pl.when(t == 1)
         def _():
             start(ins[4:6])
+            start(copies(1, 0, True, DOWNS))
 
         @pl.when(t == 2)
         def _():
             start(later)
+            start(copies(1, 1, True, DOWNS))
 
         @pl.when(t == 3)
         def _():
-            start(copies(1, 0, True, DOWNS))
-            start(copies(1, 1, True, DOWNS))
+            start(copies(1, 2, True, DOWNS))
             start([gh_cp] + ins[6:])
 
         stage_one_tile(t, xb, xf, wuo, wdo, r2)
@@ -759,7 +760,6 @@
         return carry
 
     lax.fori_loop(0, NTILE, stage_one_update, 0)
-    start(copies(1, 2, True, DOWNS))
     start(copies(1, 3, True, DOWNS))
     wait(ins[4:6])
     nw, tm[...] = update(sm[...], tm[...], gsm[D2:ROWS2, :], scal[SUB:9, 0:1])

time: 146 us -> 146 us (level)
  no operation moved by 1% of the time
where the time goes in v4:
time: 146 us
  Pallas kernels  145 us (99%)
    pallas_call x1, Pallas kernels, local_step(): got = grads_call(x_now.reshape(ROWS1, D1), labels_now, *params)  108 us
    pallas_call x1, Pallas kernels, local_step(): step_call(x_next.reshape(ROWS1, D1), *params, *vels, stack, *got[1:])  36.9 us

profile of v4, /device:TPU:0, one launch (start us, length us, event | category | flops | bytes accessed | tf_op | source)
XLA Modules:
  0.0 145.8 jit_solution(15971619503368269372)
XLA Ops:
  0.6 108.0 %grads.1 = (bf16[7,1024,512]{2,1,0:T(8,128)(2,1)S(1)}, bf16[2048,512]{1,0:T(8,128)(2,1)}, bf16[1024,512]{1,0:T(8,128)(2,1)}, f32[16,128]{1,0:T(8,128)}) custom-call(bf16[4096,128]{1,0:T(8,128)(2,1)} %bitcast.9, s32[16]{0:T(128)} %lab.1, f32[2,128,512]{2,1,0:T(8,128)} %uo_hbm.3, f32[2,512,128]{2,1,0:T(8,128)} %do_hbm.3, f32[512,512]{1,0:T(8,128)} %m_hbm.3, ...), custom_call_target="tpu_custom_call" | custom-call | tf_op jit(solution)/shard_map/grads/pallas_call | solution.py:881
  108.7 36.9 %step.1 = (f32[16,1000]{1,0:T(8,128)}, f32[2,128,512]{2,1,0:T(8,128)}, f32[2,512,128]{2,1,0:T(8,128)}, f32[512,512]{1,0:T(8,128)}, f32[2,512,2048]{2,1,0:T(8,128...) custom-call(bf16[4096,128]{1,0:T(8,128)(2,1)} %bitcast.10, ...), custom_call_target="tpu_custom_call" | custom-call | tf_op jit(solution)/shard_map/step/pallas_call | solution.py:883
